TPU v7x, 32 devices: a whole 2x2x4 slice. The times are simulated.
32 devices in a mesh: parts: 2 (over x), inner: 16 (over z, y, core).
Axes of the slice: x: 2, y: 2, z: 4, core: 2. Of those that a mesh axis runs over, the one named last changes fastest.
Arguments:
- stem_slab: bfloat16 [2, 16384, 1024], P(None, ('parts', 'inner')), parts along dimension 1, may hold values from -6 to 6
- branches: bfloat16 [3, 2, 1024, 1024], P(None, None, 'inner'), may hold values from -0.1875 to 0.1875
- column_order: int32 [3, 1024], replicated, may hold values from 0 to 1023, each once within a row
Outputs:
- result_slab: bfloat16 [2, 16384, 1024], P(None, ('parts', 'inner')), parts along dimension 1
There are 2 independent parts, one for each index of `parts`. A program takes and returns all parts, laid end to end along the dimension named above; an argument that names none is the same for every part. Nothing has to cross between parts.
Inputs may be any that keep to these rules, and one draw needn't show every extreme that they name: Each row of column_order names every number from 0 to 1023 exactly once.
All inputs are finite; a program needn't handle non-finite values.
Results may differ from a plain program's by a relative error of at most 0.0057.
Values may be sent and summed in bfloat16 or wider, within the bound.
A program may use at most 64 MiB of HBM per device.

v0:
```python
import jax
import jax.numpy as jnp
from jax import lax
from jax.sharding import PartitionSpec as P

STEPS = 3


def add_block(ordered, block_rows):
    real_part = jnp.dot(ordered[0], block_rows[0], preferred_element_type=jnp.float32) - jnp.dot(
        ordered[1], block_rows[1], preferred_element_type=jnp.float32
    )
    imag_part = jnp.dot(ordered[0], block_rows[1], preferred_element_type=jnp.float32) + jnp.dot(
        ordered[1], block_rows[0], preferred_element_type=jnp.float32
    )
    return jnp.stack([real_part, imag_part])


def folded(slab, order_row, branch_slice):
    ordered = jnp.take(slab, order_row, axis=2)
    summed = add_block(ordered, lax.all_gather(branch_slice, "inner", axis=1, tiled=True))
    return summed.astype(jnp.bfloat16)


def local(stem_slab, branches, column_order):
    current = folded(stem_slab, column_order[0], branches[0])
    for section_index in range(1, STEPS):
        current = lax.all_to_all(current, "inner", split_axis=2, concat_axis=2, tiled=True)
        current = folded(current, column_order[section_index], branches[section_index])
    return current


def solution(mesh):
    in_specs = (P(None, ("parts", "inner"), None), P(None, None, "inner", None), P())
    out_specs = P(None, ("parts", "inner"), None)
    return jax.shard_map(local, mesh=mesh, in_specs=in_specs, out_specs=out_specs, check_vma=False)
```

profile of v0, /device:TPU:13, one launch (start us, length us, event | category | flops | bytes accessed | tf_op | source)
XLA Modules:
  0.0 274.1 jit_solution(2985922748747807240)
XLA Ops:
  9.5 4.0 %copy.16 = bf16[2,512,1024]{1,0,2:T(2,128)(2,1)} copy(bf16[2,512,1024]{2,1,0:T(8,128)(2,1)S(1)} %copy-done) | data formatting | bytes 4194304 | tf_op args[0]
  13.6 7.5 %gather_fusion = bf16[1024,2,512]{2,1,0:T(2,128)(2,1)S(1)} fusion(bf16[2,512,1024]{1,0,2:T(2,128)(2,1)} %copy.16, s32[1024]{0:T(1024)S(1)} %fusion.33), kind=kCustom, calls=%fused_computation.clone | custom fusion | bytes 4198400 | tf_op jit(solution)/shard_map/jit(_take)/gather | solution.py:20
  21.1 3.9 %fusion = bf16[2,512,1024]{1,0,2:T(2,128)(2,1)S(1)} fusion(bf16[1024,2,512]{2,1,0:T(2,128)(2,1)S(1)} %gather_fusion, pred[1024]{0:T(1024)(128)(4,1)S(1)} %compare_and_fusion.2), kind=kLoop, calls=%fused_computation.21 | loop fusion | flops 1048576 | bytes 4195328 | tf_op jit(solution)/shard_map/jit(_take)/select_n | solution.py:20
  25.0 3.8 %fusion.38 = (bf16[1,512,1024]{1,0,2:T(2,128)(2,1)}, bf16[1,512,1024]{1,0,2:T(2,128)(2,1)S(1)}) fusion(bf16[2,512,1024]{1,0,2:T(2,128)(2,1)S(1)} %fusion), kind=kLoop, calls=%fused_computation.65 | loop fusion | bytes 4194304 | tf_op jit(solution)/shard_map/slice | solution.py:10
  28.8 4.6 %copy.17 = bf16[1,512,1024]{2,1,0:T(8,128)(2,1)S(1)} copy(bf16[1,512,1024]{1,0,2:T(2,128)(2,1)} %get-tuple-element.10) | data formatting | bytes 2097152 | tf_op jit(solution)/shard_map/slice | solution.py:10
  33.4 4.2 %copy.18 = bf16[1,512,1024]{2,1,0:T(8,128)(2,1)} copy(bf16[1,512,1024]{1,0,2:T(2,128)(2,1)S(1)} %get-tuple-element.11) | data formatting | bytes 2097152 | tf_op jit(solution)/shard_map/slice | solution.py:11
  37.6 23.0 %all-gather.7.cloned.1.call-done = bf16[1,2,1024,1024]{3,2,1,0:T(8,128)(2,1)} async-done(((bf16[1,2,64,1024]{3,2,1,0:T(8,128)(2,1)}), bf16[1,2,1024,1024]{3,2,1,0:T(8,128)(2,1)}) %all-gather.7.cloned.1.call-update) | async-done | bytes 4194320 | tf_op jit(solution)/shard_map/all_gather | solution.py:21
  67.7 4.0 %copy.19 = bf16[2,512,1024]{1,0,2:T(2,128)(2,1)} copy(bf16[2,512,1024]{2,1,0:T(8,128)(2,1)S(1)} %pad_maximum_fusion) | data formatting | bytes 4194304 | tf_op jit(solution)/shard_map/stack | solution.py:16
  71.7 5.5 %all-to-all-start = ((bf16[2,512,1024]{1,0,2:T(2,128)(2,1)}), bf16[2,512,1024]{1,0,2:T(2,128)(2,1)}, u32[]{:S(2)}, u32[]{:S(2)}) async-start(bf16[2,512,1024]{1,0,2:T(2,128)(2,1)} %copy.19), calls=%async_computation | async-start | bytes 4194304 | tf_op jit(solution)/shard_map/all_to_all | solution.py:28
  78.0 66.4 %all-to-all-done = bf16[2,512,1024]{1,0,2:T(2,128)(2,1)} async-done(((bf16[2,512,1024]{1,0,2:T(2,128)(2,1)}), bf16[2,512,1024]{1,0,2:T(2,128)(2,1)}, u32[]{:S(2)}, u32[]{:S(2)}) %all-to-all-start) | async-done | bytes 2097184 | tf_op jit(solution)/shard_map/all_to_all | solution.py:28
  144.3 7.5 %gather_fusion.1 = bf16[1024,2,512]{2,1,0:T(2,128)(2,1)S(1)} fusion(bf16[2,512,1024]{1,0,2:T(2,128)(2,1)} %all-to-all-done, s32[1024]{0:T(1024)S(1)} %fusion.34), kind=kCustom, calls=%fused_computation.1.clone | custom fusion | bytes 4198400 | tf_op jit(solution)/shard_map/jit(_take)/gather | solution.py:20
  151.8 3.9 %fusion.1 = bf16[2,512,1024]{1,0,2:T(2,128)(2,1)S(1)} fusion(bf16[1024,2,512]{2,1,0:T(2,128)(2,1)S(1)} %gather_fusion.1, pred[1024]{0:T(1024)(128)(4,1)S(1)} %compare_and_fusion.1), kind=kLoop, calls=%fused_computation.22 | loop fusion | flops 1048576 | bytes 4195328 | tf_op jit(solution)/shard_map/jit(_take)/select_n | solution.py:20
  155.7 3.8 %fusion.37 = (bf16[1,512,1024]{1,0,2:T(2,128)(2,1)}, bf16[1,512,1024]{1,0,2:T(2,128)(2,1)S(1)}) fusion(bf16[2,512,1024]{1,0,2:T(2,128)(2,1)S(1)} %fusion.1), kind=kLoop, calls=%fused_computation.64 | loop fusion | bytes 4194304 | tf_op jit(solution)/shard_map/slice | solution.py:10
  159.5 4.6 %copy.20 = bf16[1,512,1024]{2,1,0:T(8,128)(2,1)S(1)} copy(bf16[1,512,1024]{1,0,2:T(2,128)(2,1)} %get-tuple-element.8) | data formatting | bytes 2097152 | tf_op jit(solution)/shard_map/slice | solution.py:10
  164.1 4.2 %copy.21 = bf16[1,512,1024]{2,1,0:T(8,128)(2,1)} copy(bf16[1,512,1024]{1,0,2:T(2,128)(2,1)S(1)} %get-tuple-element.9) | data formatting | bytes 2097152 | tf_op jit(solution)/shard_map/slice | solution.py:11
  168.3 3.4 %fusion.8 = f32[512,1024]{1,0:T(8,128)S(1)} fusion(bf16[1,2,1024,1024]{3,2,1,0:T(8,128)(2,1)} %all-gather.9.cloned.1.call-done, bf16[1,512,1024]{2,1,0:T(8,128)(2,1)S(1)} %copy.20), kind=kOutput, calls=%fused_computation.29 | convolution fusion | flops 1073741824 | bytes 5242880 | tf_op jit(solution)/shard_map/dot_general | solution.py:10
  176.0 4.0 %copy.22 = bf16[2,512,1024]{1,0,2:T(2,128)(2,1)} copy(bf16[2,512,1024]{2,1,0:T(8,128)(2,1)S(1)} %pad_maximum_fusion.1) | data formatting | bytes 4194304 | tf_op jit(solution)/shard_map/stack | solution.py:16
  180.0 5.0 %all-to-all-start.1 = ((bf16[2,512,1024]{1,0,2:T(2,128)(2,1)}), bf16[2,512,1024]{1,0,2:T(2,128)(2,1)}, u32[]{:S(2)}, u32[]{:S(2)}) async-start(bf16[2,512,1024]{1,0,2:T(2,128)(2,1)} %copy.22), calls=%async_computation.1 | async-start | bytes 4194304 | tf_op jit(solution)/shard_map/all_to_all | solution.py:28
  185.1 50.1 %all-to-all-done.1 = bf16[2,512,1024]{1,0,2:T(2,128)(2,1)} async-done(((bf16[2,512,1024]{1,0,2:T(2,128)(2,1)}), bf16[2,512,1024]{1,0,2:T(2,128)(2,1)}, u32[]{:S(2)}, u32[]{:S(2)}) %all-to-all-start.1) | async-done | bytes 2097184 | tf_op jit(solution)/shard_map/all_to_all | solution.py:28
  235.1 7.5 %gather_fusion.2 = bf16[1024,2,512]{2,1,0:T(2,128)(2,1)S(1)} fusion(bf16[2,512,1024]{1,0,2:T(2,128)(2,1)} %all-to-all-done.1, s32[1024]{0:T(1024)S(1)} %fusion.35), kind=kCustom, calls=%fused_computation.2.clone | custom fusion | bytes 4198400 | tf_op jit(solution)/shard_map/jit(_take)/gather | solution.py:20
  242.6 3.9 %fusion.2 = bf16[2,512,1024]{1,0,2:T(2,128)(2,1)S(1)} fusion(bf16[1024,2,512]{2,1,0:T(2,128)(2,1)S(1)} %gather_fusion.2, pred[1024]{0:T(1024)(128)(4,1)S(1)} %compare_and_fusion), kind=kLoop, calls=%fused_computation.23 | loop fusion | flops 1048576 | bytes 4195328 | tf_op jit(solution)/shard_map/jit(_take)/select_n | solution.py:20
  246.5 3.8 %fusion.36 = (bf16[1,512,1024]{1,0,2:T(2,128)(2,1)}, bf16[1,512,1024]{1,0,2:T(2,128)(2,1)S(1)}) fusion(bf16[2,512,1024]{1,0,2:T(2,128)(2,1)S(1)} %fusion.2), kind=kLoop, calls=%fused_computation.63 | loop fusion | bytes 4194304 | tf_op jit(solution)/shard_map/slice | solution.py:10
  250.3 4.6 %copy.23 = bf16[1,512,1024]{2,1,0:T(8,128)(2,1)S(1)} copy(bf16[1,512,1024]{1,0,2:T(2,128)(2,1)} %get-tuple-element.6) | data formatting | bytes 2097152 | tf_op jit(solution)/shard_map/slice | solution.py:10
  254.9 4.2 %copy.24 = bf16[1,512,1024]{2,1,0:T(8,128)(2,1)} copy(bf16[1,512,1024]{1,0,2:T(2,128)(2,1)S(1)} %get-tuple-element.7) | data formatting | bytes 2097152 | tf_op jit(solution)/shard_map/slice | solution.py:11
  (46 shorter events, 23.4 us)
Async XLA Ops:
  6.5 3.0 %copy-start = (bf16[2,512,1024]{2,1,0:T(8,128)(2,1)S(1)}, bf16[2,512,1024]{2,1,0:T(8,128)(2,1)}, u32[]{:S(2)}) copy-start(bf16[2,512,1024]{2,1,0:T(8,128)(2,1)} %param.5) | copy-start | bytes 6291460
  6.5 54.1 %all-gather.7.cloned.1.call-start = ((), (), s32[]{:S(2)}) async-start(), calls=%async_computation.2 | async-start | bytes 4456448 | tf_op jit(solution)/shard_map/all_gather | solution.py:21
  8.8 159.5 %all-gather.9.cloned.1.call-start = ((), (), s32[]{:S(2)}) async-start(), calls=%async_computation.3 | async-start | bytes 4456448 | tf_op jit(solution)/shard_map/all_gather | solution.py:21
  9.5 4.1 %copy-start.4 = (s32[3,1024]{1,0:T(4,128)S(1)}, s32[3,1024]{1,0:T(4,128)}, u32[]{:S(2)}) copy-start(s32[3,1024]{1,0:T(4,128)} %param.7) | copy-start | bytes 36868
  37.6 26.0 %copy-start.1 = (bf16[1,512,1024]{2,1,0:T(8,128)(2,1)S(1)}, bf16[1,512,1024]{2,1,0:T(8,128)(2,1)}, u32[]{:S(2)}) copy-start(bf16[1,512,1024]{2,1,0:T(8,128)(2,1)} %copy.18) | copy-start | bytes 3145732
  60.6 3.0 %copy-start.7 = (bf16[1,2,1024,1024]{3,2,1,0:T(8,128)(2,1)S(1)}, bf16[1,2,1024,1024]{3,2,1,0:T(8,128)(2,1)}, u32[]{:S(2)}) copy-start(bf16[1,2,1024,1024]{3,2,1,0:T(8,128)(2,1)} %all-gather.7.cloned.1.call-done) | copy-start | bytes 12582916
  71.7 72.6 %all-to-all-start = ((bf16[2,512,1024]{1,0,2:T(2,128)(2,1)}), bf16[2,512,1024]{1,0,2:T(2,128)(2,1)}, u32[]{:S(2)}, u32[]{:S(2)}) async-start(bf16[2,512,1024]{1,0,2:T(2,128)(2,1)} %copy.19), calls=%async_computation | async-start | bytes 4194304 | tf_op jit(solution)/shard_map/all_to_all | solution.py:28
  77.2 181.9 %all-gather.11.cloned.1.call-start = ((), (), s32[]{:S(2)}) async-start(), calls=%async_computation.4 | async-start | bytes 4456448 | tf_op jit(solution)/shard_map/all_gather | solution.py:21
  168.3 3.4 %copy-start.2 = (bf16[1,512,1024]{2,1,0:T(8,128)(2,1)S(1)}, bf16[1,512,1024]{2,1,0:T(8,128)(2,1)}, u32[]{:S(2)}) copy-start(bf16[1,512,1024]{2,1,0:T(8,128)(2,1)} %copy.21) | copy-start | bytes 3145732
  168.3 3.6 %copy-start.5 = (bf16[1,2,1024,1024]{3,2,1,0:T(8,128)(2,1)S(1)}, bf16[1,2,1024,1024]{3,2,1,0:T(8,128)(2,1)}, u32[]{:S(2)}) copy-start(bf16[1,2,1024,1024]{3,2,1,0:T(8,128)(2,1)} %all-gather.9.cloned.1.call-done) | copy-start | bytes 12582916
  180.0 55.1 %all-to-all-start.1 = ((bf16[2,512,1024]{1,0,2:T(2,128)(2,1)}), bf16[2,512,1024]{1,0,2:T(2,128)(2,1)}, u32[]{:S(2)}, u32[]{:S(2)}) async-start(bf16[2,512,1024]{1,0,2:T(2,128)(2,1)} %copy.22), calls=%async_computation.1 | async-start | bytes 4194304 | tf_op jit(solution)/shard_map/all_to_all | solution.py:28
  259.1 3.0 %copy-start.3 = (bf16[1,512,1024]{2,1,0:T(8,128)(2,1)S(1)}, bf16[1,512,1024]{2,1,0:T(8,128)(2,1)}, u32[]{:S(2)}) copy-start(bf16[1,512,1024]{2,1,0:T(8,128)(2,1)} %copy.24) | copy-start | bytes 3145732
  259.1 3.1 %copy-start.6 = (bf16[1,2,1024,1024]{3,2,1,0:T(8,128)(2,1)S(1)}, bf16[1,2,1024,1024]{3,2,1,0:T(8,128)(2,1)}, u32[]{:S(2)}) copy-start(bf16[1,2,1024,1024]{3,2,1,0:T(8,128)(2,1)} %all-gather.11.cloned.1.call-done) | copy-start | bytes 12582916
Sparse Core Ops, SparseCore 0:
  9.5 51.0 all-gather.6
  62.8 73.3 all-gather.8
  138.4 54.5 all-gather.10
where the time goes:
time: 275 us; the launch traced here: 274 us
  waiting for transfers between devices  141 us (51%)
  local copies, waits for them, and re-layouts  74.8 us (27%)
  matrix products  20.8 us (8%)
  other arithmetic  13.7 us (5%)
  between operations  13.4 us (5%)
  starting transfers between devices  10.8 us (4%)
    all_to_all x2, waiting for transfers between devices, local(): lax.all_to_all(current, 'inner', split_axis=2, concat_axis=2, tiled=True)  116 us
    slice x6, local copies, waits for them, and re-layouts, add_block(): ordered[0]  25.1 us
    all_gather x3, waiting for transfers between devices, folded(): lax.all_gather(branch_slice, 'inner', axis=1, tiled=True)  23 us
    gather x3, local copies, waits for them, and re-layouts, folded(): ordered = jnp.take(slab, order_row, axis=2)  22.4 us
    slice x3, local copies, waits for them, and re-layouts, add_block(): ordered[1]  12.7 us
    select_n x3, other arithmetic, folded(): ordered = jnp.take(slab, order_row, axis=2)  11.8 us
    all_to_all x2, starting transfers between devices, local(): lax.all_to_all(current, 'inner', split_axis=2, concat_axis=2, tiled=True)  10.5 us
    dot_general x3, matrix products, add_block(): jnp.dot(ordered[0], block_rows[0], preferred_element_type=jnp.float32)  9.41 us
  transfers between devices with their start and end apart: 5, of which 3 were waited for; matrix products, arithmetic and copies ran while one was open for 36% of the time, Pallas kernels for 0%

commit v1 on v0

v1 whole, which is shorter than its diff:
```python
import functools

import jax
import jax.numpy as jnp
from jax import lax
from jax.experimental import pallas as pl
from jax.experimental.pallas import tpu as pltpu
from jax.sharding import PartitionSpec as P

CORES = 2
YS = 2
CHUNKS = 4
TILE = 256
LANES = 128
F32 = jnp.float32
BF16 = jnp.bfloat16
MESH_ID = pl.DeviceIdType.MESH


def add_block(ordered, block_rows):
    real_part = jnp.dot(ordered[0], block_rows[0], preferred_element_type=F32) - jnp.dot(
        ordered[1], block_rows[1], preferred_element_type=F32
    )
    imag_part = jnp.dot(ordered[0], block_rows[1], preferred_element_type=F32) + jnp.dot(
        ordered[1], block_rows[0], preferred_element_type=F32
    )
    return jnp.stack([real_part, imag_part])


def folded(slab, order_row, branch_slice):
    ordered = jnp.take(slab, order_row, axis=2)
    summed = add_block(ordered, lax.all_gather(branch_slice, "inner", axis=1, tiled=True))
    return summed.astype(BF16)


def plain(stem_slab, branches, column_order):
    current = folded(stem_slab, column_order[0], branches[0])
    for section_index in range(1, branches.shape[0]):
        current = lax.all_to_all(current, "inner", split_axis=2, concat_axis=2, tiled=True)
        current = folded(current, column_order[section_index], branches[section_index])
    return current


def kernel(
    n, stem, branches, order, out, gathered, onehot, picked, wide, send, recv,
    own_sem, zs_sem, zr_sem, ys_sem, yr_sem, cs_sem, cr_sem, as_sem, ar_sem,
):
    sections = branches.shape[0]
    depth = branches.shape[2]
    total = n * depth
    columns = branches.shape[3]
    chunk = send.shape[3]
    plane = CORES * YS
    nz = n // plane
    me = lax.axis_index("inner")
    z = me // plane
    low = me % plane
    y = low // CORES
    core = low % CORES
    y_peer = z * plane + (1 - y) * CORES + core
    core_peer = z * plane + y * CORES + (1 - core)

    barrier = pltpu.get_barrier_semaphore()

    @pl.loop(1, n)
    def _(hop):
        pl.semaphore_signal(
            barrier, inc=1, device_id={"inner": lax.rem(me + hop, n)}, device_id_type=MESH_ID
        )

    pl.semaphore_wait(barrier, n - 1)

    def remote(src, dst, send_sem, recv_sem, device):
        return pltpu.make_async_remote_copy(
            src_ref=src, dst_ref=dst, send_sem=send_sem, recv_sem=recv_sem,
            device_id={"inner": device}, device_id_type=MESH_ID,
        )

    def slot_of(zz):
        return zz * plane + low

    def own_or(s, t, slot):
        return branches.at[s] if t == 0 else gathered.at[s, slot]

    def z_copy(s, t, way):
        zz = z - t if way == 0 else z + t
        target = me + plane if way == 0 else me - plane
        slot = slot_of(zz)
        return remote(
            own_or(s, t, slot), gathered.at[s, slot], zs_sem.at[s, t, way], zr_sem.at[s, t, way], target
        )

    def z_sends(t, way):
        return (z - t >= 0) & (z + 1 < nz) if way == 0 else (z + t < nz) & (z >= 1)

    def z_holds(t, way):
        return z - t >= 0 if way == 0 else z + t < nz

    def y_copy(s, t, zz):
        slot = slot_of(zz)
        return remote(own_or(s, t, slot), gathered.at[s, slot], ys_sem.at[s, zz], yr_sem.at[s, zz], y_peer)

    def core_copy(s, t, slot):
        return remote(own_or(s, t, slot), gathered.at[s, slot], cs_sem.at[s], cr_sem.at[s], core_peer)

    def begin(s):
        for way in (0, 1):
            @pl.when(z_sends(0, way))
            def _():
                z_copy(s, 0, way).start()
        y_copy(s, 0, z).start()
        core_copy(s, 0, me).start()
        pltpu.make_async_copy(branches.at[s], gathered.at[s, me], own_sem.at[s]).start()

    def z_step(s, t):
        for way in (0, 1):
            zz = z - t if way == 0 else z + t

            @pl.when(z_holds(t, way))
            def _():
                slot = slot_of(zz)
                remote(
                    gathered.at[s, slot], gathered.at[s, slot], zs_sem.at[s, t - 1, way],
                    zr_sem.at[s, t - 1, way], y_peer,
                ).wait_recv()

                if t < nz - 1:
                    @pl.when(z_sends(t, way))
                    def _():
                        z_copy(s, t, way).start()

                y_copy(s, t, zz).start()
                core_copy(s, t, slot).start()

    def y_step(s, t):
        ways = (0,) if t == 0 else (0, 1)
        for way in ways:
            zz = z - t if way == 0 else z + t

            @pl.when(z_holds(t, way))
            def _():
                slot = zz * plane + (1 - y) * CORES + core
                remote(
                    gathered.at[s, slot], gathered.at[s, slot], ys_sem.at[s, zz], yr_sem.at[s, zz], y_peer
                ).wait_recv()
                core_copy(s, 1, slot).start()

    def finish(s):
        half = gathered.at[s, pl.ds(0, n // CORES)]
        remote(half, half, cs_sem.at[s], cr_sem.at[s], core_peer).wait_recv()
        pltpu.make_async_copy(branches.at[s], gathered.at[s, me], own_sem.at[s]).wait()

    def build_onehot(s):
        @pl.loop(0, total // LANES)
        def _(i):
            rows = pl.ds(pl.multiple_of(i * LANES, LANES), LANES)
            target = lax.broadcasted_iota(jnp.int32, (LANES, total), 0) + i * LANES
            onehot[rows, :] = jnp.where(order[s : s + 1, :] == target, 1.0, 0.0).astype(BF16)

    def pick_stem():
        @pl.loop(0, total // TILE)
        def _(j):
            cols = pl.ds(pl.multiple_of(j * TILE, TILE), TILE)
            for p in range(2):
                picked[p, :, cols] = jnp.dot(
                    stem[p], onehot[:, cols], preferred_element_type=F32
                ).astype(BF16)

    def prepare(s):
        build_onehot(s)
        groups = TILE // depth

        @pl.loop(0, columns // TILE)
        def _(j):
            cols = pl.ds(pl.multiple_of(j * TILE, TILE), TILE)
            real_rows = gathered[s, :, 0, :, cols].reshape(total, TILE)
            imag_rows = gathered[s, :, 1, :, cols].reshape(total, TILE)
            for i in range(total // TILE):
                rows = onehot[i * TILE : (i + 1) * TILE, :]
                real = jnp.dot(rows, real_rows, preferred_element_type=F32)
                imag = jnp.dot(rows, imag_rows, preferred_element_type=F32)
                real_b = real.astype(BF16)
                imag_b = imag.astype(BF16)
                minus_b = (-imag).astype(BF16)
                for b in range(groups):
                    part = slice(b * depth, (b + 1) * depth)
                    at = (i * groups + b) * 2 * depth
                    wide[s - 1, 0, at : at + depth, cols] = real_b[part]
                    wide[s - 1, 0, at + depth : at + 2 * depth, cols] = minus_b[part]
                    wide[s - 1, 1, at : at + depth, cols] = imag_b[part]
                    wide[s - 1, 1, at + depth : at + 2 * depth, cols] = real_b[part]

    low_half = lax.broadcasted_iota(jnp.int32, (chunk, LANES), 1) < LANES // 2

    def pack(step, k, j, real, imag):
        for t in range(TILE // LANES):
            re = real[:, t * LANES : (t + 1) * LANES]
            im = imag[:, t * LANES : (t + 1) * LANES]
            first = jnp.where(low_half, re, pltpu.roll(im, LANES // 2, 1))
            second = jnp.where(low_half, pltpu.roll(re, LANES // 2, 1), im)
            base = (j * (TILE // LANES) + t) * 2
            send[step, k, base] = first.astype(BF16)
            send[step, k, base + 1] = second.astype(BF16)

    def swap_start(step, k):
        recv[step, k, me] = send[step, k, me]

        @pl.loop(1, n)
        def _(hop):
            target = lax.rem(me + hop, n)
            remote(
                send.at[step, k, target], recv.at[step, k, me], as_sem.at[step, k], ar_sem.at[step, k], target
            ).start()

    def swap_wait(step, k):
        part = pl.ds(0, n - 1)
        return remote(
            send.at[step, k, part], recv.at[step, k, part], as_sem.at[step, k], ar_sem.at[step, k], core_peer
        )

    def first_section(k):
        rows = slice(k * chunk, (k + 1) * chunk)

        @pl.loop(0, columns // TILE)
        def _(j):
            cols = pl.ds(pl.multiple_of(j * TILE, TILE), TILE)
            real_rows = gathered[0, :, 0, :, cols].reshape(total, TILE)
            imag_rows = gathered[0, :, 1, :, cols].reshape(total, TILE)
            a, b = picked[0, rows, :], picked[1, rows, :]
            dot = functools.partial(jnp.dot, preferred_element_type=F32)
            pack(0, k, j, dot(a, real_rows) - dot(b, imag_rows), dot(a, imag_rows) + dot(b, real_rows))

    def later_section(s, k):
        rows = slice(k * chunk, (k + 1) * chunk)

        @pl.loop(0, columns // TILE)
        def _(j):
            cols = pl.ds(pl.multiple_of(j * TILE, TILE), TILE)
            left = jnp.concatenate([recv[s - 1, k, g] for g in range(n)], axis=1)
            real = jnp.dot(left, wide[s - 1, 0, :, cols], preferred_element_type=F32)
            imag = jnp.dot(left, wide[s - 1, 1, :, cols], preferred_element_type=F32)
            if s < sections - 1:
                pack(s, k, j, real, imag)
            else:
                out[0, rows, cols] = real.astype(BF16)
                out[1, rows, cols] = imag.astype(BF16)

    begin(0)
    build_onehot(0)
    pick_stem()
    z_step(0, 1)
    y_step(0, 0)
    begin(1)
    for t in range(2, nz):
        z_step(0, t)
        y_step(0, t - 1)
        z_step(1, t - 1)
    begin(2)
    y_step(0, nz - 1)
    finish(0)
    for k in range(CHUNKS):
        first_section(k)
        swap_start(0, k)
    z_step(1, nz - 1)
    for t in range(nz):
        y_step(1, t)
    for t in range(1, nz):
        z_step(2, t)
    finish(1)
    prepare(1)
    for k in range(CHUNKS):
        swap_wait(0, k).wait_recv()
        later_section(1, k)
        swap_start(1, k)
        if k == CHUNKS // 2:
            for t in range(nz):
                y_step(2, t)
            finish(2)
            prepare(2)
    for k in range(CHUNKS):
        swap_wait(1, k).wait_recv()
        later_section(2, k)

    for step in range(sections - 1):
        for k in range(CHUNKS):
            swap_wait(step, k).wait_send()
    for s in range(sections):
        for t in range(nz - 1):
            for way in (0, 1):
                @pl.when(z_sends(t, way))
                def _():
                    z_copy(s, t, way).wait_send()
        for zz in range(nz):
            y_copy(s, 1, zz).wait_send()
        half = gathered.at[s, pl.ds(0, n // CORES)]
        remote(half, half, cs_sem.at[s], cr_sem.at[s], core_peer).wait_send()


def fused(n, stem_slab, branches, column_order):
    sections, _, depth, columns = branches.shape
    rows = stem_slab.shape[1]
    chunk = rows // CHUNKS
    nz = n // (CORES * YS)
    total = n * depth
    dma = pltpu.SemaphoreType.DMA
    return pl.pallas_call(
        functools.partial(kernel, n),
        out_shape=jax.ShapeDtypeStruct(stem_slab.shape, BF16),
        in_specs=[pl.BlockSpec(memory_space=pltpu.VMEM)] * 3,
        out_specs=pl.BlockSpec(memory_space=pltpu.VMEM),
        scratch_shapes=[
            pltpu.VMEM((sections, n, 2, depth, columns), BF16),
            pltpu.VMEM((total, total), BF16),
            pltpu.VMEM(stem_slab.shape, BF16),
            pltpu.VMEM((sections - 1, 2, 2 * total, columns), BF16),
            pltpu.VMEM((sections - 1, CHUNKS, n, chunk, LANES), BF16),
            pltpu.VMEM((sections - 1, CHUNKS, n, chunk, LANES), BF16),
            dma((sections,)),
            dma((sections, nz, 2)),
            dma((sections, nz, 2)),
            dma((sections, nz)),
            dma((sections, nz)),
            dma((sections,)),
            dma((sections,)),
            dma((sections - 1, CHUNKS)),
            dma((sections - 1, CHUNKS)),
        ],
        compiler_params=pltpu.CompilerParams(
            collective_id=0, has_side_effects=True, vmem_limit_bytes=60 * 2**20
        ),
    )(stem_slab, branches, column_order)


def solution(mesh):
    n = mesh.shape["inner"]

    def local(stem_slab, branches, column_order):
        columns = branches.shape[3]
        fits = 2 * (columns // n) == LANES and n % (CORES * YS) == 0 and n > CORES * YS
        if fits and branches.shape[0] == 3 and columns == n * branches.shape[2]:
            return fused(n, stem_slab, branches, column_order)
        return plain(stem_slab, branches, column_order)

    in_specs = (P(None, ("parts", "inner"), None), P(None, None, "inner", None), P())
    out_specs = P(None, ("parts", "inner"), None)
    return jax.shard_map(local, mesh=mesh, in_specs=in_specs, out_specs=out_specs, check_vma=False)
```

time: 275 us -> 157 us (0.57)
  Pallas kernels: 0 us -> 153 us
  waiting for transfers between devices: 141 us -> 0 us
  local copies, waits for them, and re-layouts: 74.8 us -> 3.08 us
  matrix products: 20.8 us -> 0 us
  other arithmetic: 13.7 us -> 0 us
  between operations: 13.4 us -> 0.01 us
  starting transfers between devices: 10.8 us -> 0 us
    pallas_call x0 -> x1, Pallas kernels: none -> 153 us  [fused(): pl.pallas_call(functools.partial(kernel, n), out_shape=jax.ShapeDtypeStru...]
    all_to_all x2 -> x0, waiting for transfers between devices: 116 us -> none  [local(): lax.all_to_all(current, 'inner', split_axis=2, concat_axis=2, tiled=True)]
    slice x11 -> x0, local copies, waits for them, and re-layouts: 40 us -> none  [the longest x6 25.1 us: add_block(): ordered[0]]
    all_gather x3 -> x0, waiting for transfers between devices: 23 us -> none  [folded(): lax.all_gather(branch_slice, 'inner', axis=1, tiled=True)]
    gather x3 -> x0, local copies, waits for them, and re-layouts: 22.4 us -> none  [folded(): ordered = jnp.take(slab, order_row, axis=2)]
    dot_general x12 -> x0, matrix products: 20.8 us -> none  [the longest x3 9.41 us: add_block(): jnp.dot(ordered[0], block_rows[0], preferred_element_type=jnp.float32)]
    select_n x3 -> x0, other arithmetic: 11.8 us -> none  [folded(): ordered = jnp.take(slab, order_row, axis=2)]
    all_to_all x2 -> x0, starting transfers between devices: 10.5 us -> none  [local(): lax.all_to_all(current, 'inner', split_axis=2, concat_axis=2, tiled=True)]
  transfers between devices with their start and end apart: 5 -> 0, of which waited for: 3 -> 0; matrix products, arithmetic and copies ran while one was open for 36% -> 0% of each run, Pallas kernels for 0% -> 0%
where the time goes in v1:
time: 157 us; the launch traced here: 156 us
  Pallas kernels  153 us (97%)
  local copies, waits for them, and re-layouts  3.08 us (2%)
    pallas_call x1, Pallas kernels, fused(): pl.pallas_call(functools.partial(kernel, n), out_shape=jax.ShapeDtypeStru...  153 us

profile of v1, /device:TPU:13, one launch (start us, length us, event | category | flops | bytes accessed | tf_op | source)
XLA Modules:
  0.0 156.3 jit_solution(15864311372347172814)
XLA Ops:
  0.0 153.2 %shard_map.37 = bf16[2,512,1024]{2,1,0:T(8,128)(2,1)} custom-call(bf16[2,512,1024]{2,1,0:T(8,128)(2,1)} %stem.1, bf16[3,2,64,1024]{3,2,1,0:T(8,128)(2,1)} %branches.1, s32[3,1024]{1,0:T(4,128)} %order.1), custom_call_target="tpu_custom_call" | custom-call | tf_op jit(solution)/shard_map/pallas_call | solution.py:306
  153.2 3.1 %copy.5 = bf16[2,512,1024]{2,1,0:T(8,128)(2,1)} copy(bf16[2,512,1024]{2,1,0:T(8,128)(2,1)} %shard_map.37) | data formatting | bytes 4194304

commit v2 on v1

--- a/solution.py
+++ b/solution.py
@@ -42,8 +42,9 @@
 
 
 def kernel(
-    n, stem, branches, order, out, gathered, onehot, picked, wide, send, recv,
-    own_sem, zs_sem, zr_sem, ys_sem, yr_sem, cs_sem, cr_sem, as_sem, ar_sem,
+    n, stem_hbm, branches, order, out_hbm, stem, out, gathered, onehot, picked, wide, send, recv,
+    own_sem, zs_sem, zr_sem, xs_sem, xr_sem, ys_sem, yr_sem, ds_sem, dr_sem, cs_sem, cr_sem, as_sem, ar_sem,
+    in_sem, out_sem,
 ):
     sections = branches.shape[0]
     depth = branches.shape[2]
@@ -53,12 +54,18 @@
     plane = CORES * YS
     nz = n // plane
     me = lax.axis_index("inner")
+    x = lax.axis_index("parts")
     z = me // plane
     low = me % plane
     y = low // CORES
     core = low % CORES
-    y_peer = z * plane + (1 - y) * CORES + core
-    core_peer = z * plane + y * CORES + (1 - core)
+    other_low = (1 - y) * CORES + core
+    x_peer = {"parts": 1 - x}
+    y_peer = {"inner": z * plane + other_low}
+    core_peer = {"inner": z * plane + y * CORES + (1 - core)}
+
+    stem_copy = pltpu.make_async_copy(stem_hbm, stem, in_sem)
+    stem_copy.start()
 
     barrier = pltpu.get_barrier_semaphore()
 
@@ -68,27 +75,26 @@
             barrier, inc=1, device_id={"inner": lax.rem(me + hop, n)}, device_id_type=MESH_ID
         )
 
-    pl.semaphore_wait(barrier, n - 1)
+    pl.semaphore_signal(barrier, inc=1, device_id=x_peer, device_id_type=MESH_ID)
+    pl.semaphore_wait(barrier, n)
 
     def remote(src, dst, send_sem, recv_sem, device):
         return pltpu.make_async_remote_copy(
             src_ref=src, dst_ref=dst, send_sem=send_sem, recv_sem=recv_sem,
-            device_id={"inner": device}, device_id_type=MESH_ID,
+            device_id=device, device_id_type=MESH_ID,
         )
 
-    def slot_of(zz):
-        return zz * plane + low
-
-    def own_or(s, t, slot):
-        return branches.at[s] if t == 0 else gathered.at[s, slot]
+    def block(s, zz, across, p, own=False):
+        slot = zz * plane + (other_low if across else low)
+        return (branches.at[s, p] if own else gathered.at[s, slot, p]), gathered.at[s, slot, p]
+
+    def z_of(t, way):
+        return z - t if way == 0 else z + t
 
     def z_copy(s, t, way):
-        zz = z - t if way == 0 else z + t
-        target = me + plane if way == 0 else me - plane
-        slot = slot_of(zz)
-        return remote(
-            own_or(s, t, slot), gathered.at[s, slot], zs_sem.at[s, t, way], zr_sem.at[s, t, way], target
-        )
+        src, dst = block(s, z_of(t, way), False, x, own=t == 0)
+        target = {"inner": me + plane if way == 0 else me - plane}
+        return remote(src, dst, zs_sem.at[s, t, way], zr_sem.at[s, t, way], target)
 
     def z_sends(t, way):
         return (z - t >= 0) & (z + 1 < nz) if way == 0 else (z + t < nz) & (z >= 1)
@@ -96,54 +102,95 @@
     def z_holds(t, way):
         return z - t >= 0 if way == 0 else z + t < nz
 
-    def y_copy(s, t, zz):
-        slot = slot_of(zz)
-        return remote(own_or(s, t, slot), gathered.at[s, slot], ys_sem.at[s, zz], yr_sem.at[s, zz], y_peer)
-
-    def core_copy(s, t, slot):
-        return remote(own_or(s, t, slot), gathered.at[s, slot], cs_sem.at[s], cr_sem.at[s], core_peer)
-
-    def begin(s):
+    def x_copy(s, zz):
+        src, dst = block(s, zz, False, x)
+        return remote(src, dst, xs_sem.at[s, zz], xr_sem.at[s, zz], x_peer)
+
+    def y_copy(s, zz, own=False):
+        src, dst = block(s, zz, False, x, own)
+        return remote(src, dst, ys_sem.at[s, zz], yr_sem.at[s, zz], y_peer)
+
+    def diagonal_x(s, zz):
+        src, dst = block(s, zz, True, x)
+        return remote(src, dst, ds_sem.at[s, zz], dr_sem.at[s, zz], x_peer)
+
+    def diagonal_y(s, zz, own=False):
+        src, dst = block(s, zz, False, 1 - x, own)
+        return remote(src, dst, ds_sem.at[s, zz], dr_sem.at[s, zz], y_peer)
+
+    def core_send(s, zz, across, p, own=False):
+        src, dst = block(s, zz, across, p, own)
+        remote(src, dst, cs_sem.at[s], cr_sem.at[s], core_peer).start()
+
+    def arrived(s, zz, across, p, sem):
+        _, dst = block(s, zz, across, p)
+        remote(dst, dst, cs_sem.at[s], sem, core_peer).wait_recv()
+
+    def begin_z(s):
         for way in (0, 1):
             @pl.when(z_sends(0, way))
             def _():
                 z_copy(s, 0, way).start()
-        y_copy(s, 0, z).start()
-        core_copy(s, 0, me).start()
+
+    def begin_side(s):
+        y_copy(s, z, own=True).start()
+
+        @pl.when(core == 1)
+        def _():
+            diagonal_y(s, z, own=True).start()
+
+        core_send(s, z, False, x, own=True)
+        core_send(s, z, False, 1 - x, own=True)
         pltpu.make_async_copy(branches.at[s], gathered.at[s, me], own_sem.at[s]).start()
 
     def z_step(s, t):
         for way in (0, 1):
-            zz = z - t if way == 0 else z + t
-
             @pl.when(z_holds(t, way))
             def _():
-                slot = slot_of(zz)
-                remote(
-                    gathered.at[s, slot], gathered.at[s, slot], zs_sem.at[s, t - 1, way],
-                    zr_sem.at[s, t - 1, way], y_peer,
-                ).wait_recv()
+                arrived(s, z_of(t, way), False, x, zr_sem.at[s, t - 1, way])
 
                 if t < nz - 1:
                     @pl.when(z_sends(t, way))
                     def _():
                         z_copy(s, t, way).start()
 
-                y_copy(s, t, zz).start()
-                core_copy(s, t, slot).start()
-
-    def y_step(s, t):
-        ways = (0,) if t == 0 else (0, 1)
-        for way in ways:
-            zz = z - t if way == 0 else z + t
-
+    def side_send(s, t):
+        for way in (0, 1):
             @pl.when(z_holds(t, way))
             def _():
-                slot = zz * plane + (1 - y) * CORES + core
-                remote(
-                    gathered.at[s, slot], gathered.at[s, slot], ys_sem.at[s, zz], yr_sem.at[s, zz], y_peer
-                ).wait_recv()
-                core_copy(s, 1, slot).start()
+                zz = z_of(t, way)
+                x_copy(s, zz).start()
+                y_copy(s, zz).start()
+                core_send(s, zz, False, x)
+
+    def side_step(s, t):
+        for way in (0,) if t == 0 else (0, 1):
+            @pl.when(z_holds(t, way))
+            def _():
+                zz = z_of(t, way)
+                arrived(s, zz, True, x, yr_sem.at[s, zz])
+
+                @pl.when(core == 0)
+                def _():
+                    diagonal_x(s, zz).start()
+
+                core_send(s, zz, True, x)
+                if t > 0:
+                    arrived(s, zz, False, 1 - x, xr_sem.at[s, zz])
+
+                    @pl.when(core == 1)
+                    def _():
+                        diagonal_y(s, zz).start()
+
+                    core_send(s, zz, False, 1 - x)
+
+    def diagonal_step(s, t):
+        for way in (0,) if t == 0 else (0, 1):
+            @pl.when(z_holds(t, way))
+            def _():
+                zz = z_of(t, way)
+                arrived(s, zz, True, 1 - x, dr_sem.at[s, zz])
+                core_send(s, zz, True, 1 - x)
 
     def finish(s):
         half = gathered.at[s, pl.ds(0, n // CORES)]
@@ -209,7 +256,8 @@
         def _(hop):
             target = lax.rem(me + hop, n)
             remote(
-                send.at[step, k, target], recv.at[step, k, me], as_sem.at[step, k], ar_sem.at[step, k], target
+                send.at[step, k, target], recv.at[step, k, me], as_sem.at[step, k], ar_sem.at[step, k],
+                {"inner": target},
             ).start()
 
     def swap_wait(step, k):
@@ -245,41 +293,66 @@
                 out[0, rows, cols] = real.astype(BF16)
                 out[1, rows, cols] = imag.astype(BF16)
 
-    begin(0)
+    def out_copy(k):
+        rows = slice(k * chunk, (k + 1) * chunk)
+        return pltpu.make_async_copy(out.at[:, rows], out_hbm.at[:, rows], out_sem.at[k])
+
+    begin_z(0)
+    begin_side(0)
     build_onehot(0)
+    stem_copy.wait()
     pick_stem()
-    z_step(0, 1)
-    y_step(0, 0)
-    begin(1)
-    for t in range(2, nz):
+    for t in range(1, nz):
         z_step(0, t)
-        y_step(0, t - 1)
-        z_step(1, t - 1)
-    begin(2)
-    y_step(0, nz - 1)
+        side_send(0, t)
+        if t == 1:
+            begin_z(1)
+        else:
+            z_step(1, t - 1)
+        if t == nz - 1:
+            begin_z(2)
+        side_step(0, t - 1)
+        if t >= 2:
+            diagonal_step(0, t - 2)
+    side_step(0, nz - 1)
+    z_step(1, nz - 1)
+    diagonal_step(0, nz - 2)
+    z_step(2, 1)
+    diagonal_step(0, nz - 1)
+    begin_side(1)
+    for t in range(1, nz):
+        side_send(1, t)
     finish(0)
     for k in range(CHUNKS):
         first_section(k)
         swap_start(0, k)
-    z_step(1, nz - 1)
+        if k == 0:
+            for t in range(2, nz):
+                z_step(2, t)
     for t in range(nz):
-        y_step(1, t)
+        side_step(1, t)
+    for t in range(nz):
+        diagonal_step(1, t)
+    begin_side(2)
     for t in range(1, nz):
-        z_step(2, t)
+        side_send(2, t)
     finish(1)
     prepare(1)
     for k in range(CHUNKS):
         swap_wait(0, k).wait_recv()
         later_section(1, k)
         swap_start(1, k)
-        if k == CHUNKS // 2:
+        if k == CHUNKS - 2:
             for t in range(nz):
-                y_step(2, t)
-            finish(2)
-            prepare(2)
+                side_step(2, t)
+            for t in range(nz):
+                diagonal_step(2, t)
+    finish(2)
+    prepare(2)
     for k in range(CHUNKS):
         swap_wait(1, k).wait_recv()
         later_section(2, k)
+        out_copy(k).start()
 
     for step in range(sections - 1):
         for k in range(CHUNKS):
@@ -291,9 +364,16 @@
                 def _():
                     z_copy(s, t, way).wait_send()
         for zz in range(nz):
-            y_copy(s, 1, zz).wait_send()
+            @pl.when(z != zz)
+            def _():
+                x_copy(s, zz).wait_send()
+
+            y_copy(s, zz).wait_send()
+            diagonal_y(s, zz).wait_send()
         half = gathered.at[s, pl.ds(0, n // CORES)]
         remote(half, half, cs_sem.at[s], cr_sem.at[s], core_peer).wait_send()
+    for k in range(CHUNKS):
+        out_copy(k).wait()
 
 
 def fused(n, stem_slab, branches, column_order):
@@ -306,9 +386,11 @@
     return pl.pallas_call(
         functools.partial(kernel, n),
         out_shape=jax.ShapeDtypeStruct(stem_slab.shape, BF16),
-        in_specs=[pl.BlockSpec(memory_space=pltpu.VMEM)] * 3,
-        out_specs=pl.BlockSpec(memory_space=pltpu.VMEM),
+        in_specs=[pl.BlockSpec(memory_space=pl.ANY)] + [pl.BlockSpec(memory_space=pltpu.VMEM)] * 2,
+        out_specs=pl.BlockSpec(memory_space=pl.ANY),
         scratch_shapes=[
+            pltpu.VMEM(stem_slab.shape, BF16),
+            pltpu.VMEM(stem_slab.shape, BF16),
             pltpu.VMEM((sections, n, 2, depth, columns), BF16),
             pltpu.VMEM((total, total), BF16),
             pltpu.VMEM(stem_slab.shape, BF16),
@@ -318,12 +400,13 @@
             dma((sections,)),
             dma((sections, nz, 2)),
             dma((sections, nz, 2)),
-            dma((sections, nz)),
-            dma((sections, nz)),
+            *[dma((sections, nz))] * 6,
             dma((sections,)),
             dma((sections,)),
             dma((sections - 1, CHUNKS)),
             dma((sections - 1, CHUNKS)),
+            dma,
+            dma((CHUNKS,)),
         ],
         compiler_params=pltpu.CompilerParams(
             collective_id=0, has_side_effects=True, vmem_limit_bytes=60 * 2**20
@@ -336,7 +419,7 @@
 
     def local(stem_slab, branches, column_order):
         columns = branches.shape[3]
-        fits = 2 * (columns // n) == LANES and n % (CORES * YS) == 0 and n > CORES * YS
+        fits = mesh.shape["parts"] == 2 and 2 * (columns // n) == LANES and n % (CORES * YS) == 0 and n > CORES * YS
         if fits and branches.shape[0] == 3 and columns == n * branches.shape[2]:
             return fused(n, stem_slab, branches, column_order)
         return plain(stem_slab, branches, column_order)

time: 157 us -> 130 us (0.83)
  Pallas kernels: 153 us -> 126 us
    pallas_call x1, Pallas kernels: 153 us -> 126 us  [fused(): pl.pallas_call(functools.partial(kernel, n), out_shape=jax.ShapeDtypeStru...]
where the time goes in v2:
time: 130 us; the launch traced here: 129 us
  Pallas kernels  126 us (97%)
  local copies, waits for them, and re-layouts  3.08 us (2%)
    pallas_call x1, Pallas kernels, fused(): pl.pallas_call(functools.partial(kernel, n), out_shape=jax.ShapeDtypeStru...  126 us
    unnamed x1, local copies, waits for them, and re-layouts  3.08 us

profile of v2, /device:TPU:13, one launch (start us, length us, event | category | flops | bytes accessed | tf_op | source)
XLA Modules:
  0.0 128.9 jit_solution(12142860659103410527)
XLA Ops:
  0.0 125.8 %shard_map.37 = bf16[2,512,1024]{2,1,0:T(8,128)(2,1)} custom-call(bf16[2,512,1024]{2,1,0:T(8,128)(2,1)} %stem_hbm.1, bf16[3,2,64,1024]{3,2,1,0:T(8,128)(2,1)} %branches.1, s32[3,1024]{1,0:T(4,128)} %order.1), custom_call_target="tpu_custom_call" | custom-call | tf_op jit(solution)/shard_map/pallas_call | solution.py:386
  125.8 3.1 %copy.5 = bf16[2,512,1024]{2,1,0:T(8,128)(2,1)} copy(bf16[2,512,1024]{2,1,0:T(8,128)(2,1)} %shard_map.37) | data formatting | bytes 4194304
